TPU v7x, 32 devices: a whole 2x2x4 slice. The times are simulated.
32 devices in a mesh: shard: 4 (over z), replica: 8 (over y, x, core).
Axes of the slice: x: 2, y: 2, z: 4, core: 2. Of those that a mesh axis runs over, the one named last changes fastest.
Arguments:
- block_in: bfloat16 [4096, 2048], P(('shard', 'replica')), may hold values from -6 to 6
- positions: int32 [4096], P(('shard', 'replica')), may hold values from 0 to 127, as said below
- out_grad: bfloat16 [4096, 2048], P(('shard', 'replica')), may hold values from -6 to 6
- w_qkv: bfloat16 [2048, 6144], P('shard'), may hold values from -0.125 to 0.125
- b_qkv: bfloat16 [6144], P('shard'), may hold values from -4.75 to 4.75
- w_out: bfloat16 [2048, 2048], P('shard'), may hold values from -0.25 to 0.25
- b_out: bfloat16 [2048], P('shard'), may hold values from -3 to 3
- w_up: bfloat16 [2048, 8192], P('shard'), may hold values from -0.125 to 0.125
- b_up: bfloat16 [8192], P('shard'), may hold values from -3 to 3
- w_down: bfloat16 [8192, 2048], P('shard'), may hold values from -0.0625 to 0.0625
- b_down: bfloat16 [2048], P('shard'), may hold values from -3 to 3
- first_gain: bfloat16 [2048], P('shard'), may hold values from 0.5 to 1.5
- first_shift: bfloat16 [2048], P('shard'), may hold values from -3 to 3
- second_gain: bfloat16 [2048], P('shard'), may hold values from 0.5 to 1.5
- second_shift: bfloat16 [2048], P('shard'), may hold values from -3 to 3
Outputs:
- block_out: bfloat16 [4096, 2048], P(('shard', 'replica'))
- in_grad: bfloat16 [4096, 2048], P(('shard', 'replica'))
- grad_w_qkv: float32 [2048, 6144], P('shard')
- grad_b_qkv: float32 [6144], P('shard')
- grad_w_out: float32 [2048, 2048], P('shard')
- grad_b_out: float32 [2048], P('shard')
- grad_w_up: float32 [2048, 8192], P('shard')
- grad_b_up: float32 [8192], P('shard')
- grad_w_down: float32 [8192, 2048], P('shard')
- grad_b_down: float32 [2048], P('shard')
- grad_first_gain: float32 [2048], P('shard')
- grad_first_shift: float32 [2048], P('shard')
- grad_second_gain: float32 [2048], P('shard')
- grad_second_shift: float32 [2048], P('shard')
Inputs may be any that keep to these rules, and one draw needn't show every extreme that they name: `positions`: each device's 128 tokens hold whole sequences: a position is 0 at a sequence's start and at each device's first token and otherwise one more than the position before; some device holds one sequence of 128 tokens.
All inputs are finite; a program needn't handle non-finite values.
Results may differ from a plain program's by a relative error of at most 0.006.
The roundings to bfloat16 on the way count: a program that leaves them out, or rounds other values in their place, can miss the bound.
Values may be sent and summed in bfloat16 or wider, within the bound.
A program may use at most 384 MiB of HBM per device.

v0:
```python
import jax
import jax.numpy as jnp
from jax import lax
from jax.sharding import PartitionSpec as P

D = 2048
H = 8
HD = 256
ROT = 64
epsilon = 1e-05


def norm_forward(values, gain, shift):
    centre = jnp.mean(values, axis=-1, keepdims=True)
    offsets = values - centre
    spread = jnp.mean(offsets * offsets, axis=-1, keepdims=True)
    inverse = lax.rsqrt(spread + epsilon)
    normed = offsets * inverse
    return (normed * gain.astype(jnp.float32) + shift.astype(jnp.float32), normed, inverse)


def norm_backward(upstream, normed, inverse, gain):
    scaled = upstream * gain.astype(jnp.float32)
    inward = inverse * (
        scaled
        - jnp.mean(scaled, axis=-1, keepdims=True)
        - normed * jnp.mean(scaled * normed, axis=-1, keepdims=True)
    )
    return (inward, jnp.sum(upstream * normed, axis=0), jnp.sum(upstream, axis=0))


def rotary_tables(positions):
    half_rot = ROT // 2
    freqs = 10000.0 ** (-(jnp.arange(half_rot, dtype=jnp.float32) * (2.0 / ROT)))
    angles = positions.astype(jnp.float32)[:, None] * freqs[None, :]
    return (jnp.cos(angles)[:, None, :], jnp.sin(angles)[:, None, :])


def rotate(values, cosine, sine):
    half_rot = ROT // 2
    first = values[..., :half_rot]
    second = values[..., half_rot:ROT]
    return jnp.concatenate(
        [first * cosine - second * sine, second * cosine + first * sine, values[..., ROT:]], axis=-1
    )


def gelu_value(values):
    return 0.5 * values * (1.0 + lax.erf(values * 0.7071067811865476))


def gelu_slope(values):
    return (
        0.5 * (1.0 + lax.erf(values * 0.7071067811865476))
        + values * jnp.exp(-0.5 * values * values) * 0.3989422804014327
    )


def contract_rows(left, right):
    return lax.dot_general(
        left, right, (((0,), (0,)), ((), ())), preferred_element_type=jnp.float32
    )


def times_transpose(left, right):
    return lax.dot_general(
        left, right, (((1,), (1,)), ((), ())), preferred_element_type=jnp.float32
    )


def causal_mask(positions):
    count = positions.shape[0]
    index = jnp.arange(count, dtype=jnp.int32)
    behind = index[:, None] - index[None, :]
    return (behind >= 0) & (behind <= positions[:, None])


def attend_forward(queries, keys, values, positions):
    allowed = causal_mask(positions)[None]
    scale = HD ** (-0.5)
    scores = jnp.einsum("qhd,khd->hqk", queries, keys, preferred_element_type=jnp.float32) * scale
    scores = jnp.where(allowed, scores, -1e30)
    peak = jnp.max(scores, axis=-1, keepdims=True)
    logsum = peak + jnp.log(jnp.sum(jnp.exp(scores - peak), axis=-1, keepdims=True))
    probs = jnp.exp(scores - logsum).astype(jnp.bfloat16)
    outputs = jnp.einsum("hqk,khd->qhd", probs, values, preferred_element_type=jnp.float32).astype(
        jnp.bfloat16
    )
    return (outputs.reshape(queries.shape[0], D), logsum[..., 0])


def attend_backward(queries, keys, values, attended_grad, logsums, positions):
    allowed = causal_mask(positions)[None]
    scale = HD ** (-0.5)
    upstream = attended_grad.reshape(queries.shape[0], H, HD)
    scores = jnp.einsum("qhd,khd->hqk", queries, keys, preferred_element_type=jnp.float32) * scale
    scores = jnp.where(allowed, scores, -1e30)
    probs = jnp.exp(scores - logsums[..., None])
    probs_low = probs.astype(jnp.bfloat16)
    dprobs = jnp.einsum("qhd,khd->hqk", upstream, values, preferred_element_type=jnp.float32)
    total = jnp.sum(probs * dprobs, axis=-1, keepdims=True)
    dscores = (probs * (dprobs - total) * scale).astype(jnp.bfloat16)
    query_grad = jnp.einsum("hqk,khd->qhd", dscores, keys, preferred_element_type=jnp.float32)
    key_grad = jnp.einsum("hqk,qhd->khd", dscores, queries, preferred_element_type=jnp.float32)
    value_grad = jnp.einsum("hqk,qhd->khd", probs_low, upstream, preferred_element_type=jnp.float32)
    return (query_grad, key_grad, value_grad)


def layer_forward(block_in, positions, params):
    (
        w_qkv,
        b_qkv,
        w_out,
        b_out,
        w_up,
        b_up,
        w_down,
        b_down,
        first_gain,
        first_shift,
        second_gain,
        second_shift,
    ) = params
    count = block_in.shape[0]
    wide_in = block_in.astype(jnp.float32)
    first_full, first_normed, first_inverse = norm_forward(wide_in, first_gain, first_shift)
    second_full, second_normed, second_inverse = norm_forward(wide_in, second_gain, second_shift)
    first_low = first_full.astype(jnp.bfloat16)
    second_low = second_full.astype(jnp.bfloat16)
    mixed = jnp.dot(first_low, w_qkv, preferred_element_type=jnp.float32) + b_qkv.astype(
        jnp.float32
    )
    cosine, sine = rotary_tables(positions)
    queries = rotate(mixed[:, :D].reshape(count, H, HD), cosine, sine).astype(jnp.bfloat16)
    keys = rotate(mixed[:, D : 2 * D].reshape(count, H, HD), cosine, sine).astype(jnp.bfloat16)
    values = mixed[:, 2 * D :].reshape(count, H, HD).astype(jnp.bfloat16)
    attended, logsums = attend_forward(queries, keys, values, positions)
    branch_attn = jnp.dot(attended, w_out, preferred_element_type=jnp.float32) + b_out.astype(
        jnp.float32
    )
    hidden_pre = jnp.dot(second_low, w_up, preferred_element_type=jnp.float32) + b_up.astype(
        jnp.float32
    )
    activated = gelu_value(hidden_pre).astype(jnp.bfloat16)
    branch_ffn = jnp.dot(activated, w_down, preferred_element_type=jnp.float32) + b_down.astype(
        jnp.float32
    )
    block_out = (wide_in + branch_attn + branch_ffn).astype(jnp.bfloat16)
    saved = (
        first_normed,
        first_inverse,
        second_normed,
        second_inverse,
        first_low,
        second_low,
        queries,
        keys,
        values,
        attended,
        logsums,
        hidden_pre,
        activated,
        cosine,
        sine,
        positions,
    )
    return (block_out, saved)


def layer_backward(saved, out_grad, params):
    (
        w_qkv,
        b_qkv,
        w_out,
        b_out,
        w_up,
        b_up,
        w_down,
        b_down,
        first_gain,
        first_shift,
        second_gain,
        second_shift,
    ) = params
    (
        first_normed,
        first_inverse,
        second_normed,
        second_inverse,
        first_low,
        second_low,
        queries,
        keys,
        values,
        attended,
        logsums,
        hidden_pre,
        activated,
        cosine,
        sine,
        positions,
    ) = saved
    count = out_grad.shape[0]
    upstream = out_grad.astype(jnp.float32)
    output_sum = jnp.sum(upstream, axis=0)
    hidden_grad = times_transpose(out_grad, w_down) * gelu_slope(hidden_pre)
    grad_b_up = jnp.sum(hidden_grad, axis=0)
    hidden_low = hidden_grad.astype(jnp.bfloat16)
    second_grad = times_transpose(hidden_low, w_up)
    attended_grad = times_transpose(out_grad, w_out).astype(jnp.bfloat16)
    query_grad, key_grad, value_grad = attend_backward(
        queries, keys, values, attended_grad, logsums, positions
    )
    query_grad = rotate(query_grad, cosine, -sine)
    key_grad = rotate(key_grad, cosine, -sine)
    mixed_grad = jnp.concatenate(
        [query_grad.reshape(count, D), key_grad.reshape(count, D), value_grad.reshape(count, D)],
        axis=1,
    )
    grad_b_qkv = jnp.sum(mixed_grad, axis=0)
    mixed_low = mixed_grad.astype(jnp.bfloat16)
    first_grad = times_transpose(mixed_low, w_qkv)
    first_term, grad_first_gain, grad_first_shift = norm_backward(
        first_grad, first_normed, first_inverse, first_gain
    )
    second_term, grad_second_gain, grad_second_shift = norm_backward(
        second_grad, second_normed, second_inverse, second_gain
    )
    in_grad = (upstream + first_term + second_term).astype(jnp.bfloat16)
    small = (
        grad_b_qkv,
        output_sum,
        grad_b_up,
        output_sum,
        grad_first_gain,
        grad_first_shift,
        grad_second_gain,
        grad_second_shift,
    )
    operands = (first_low, mixed_low, attended, second_low, hidden_low, activated)
    return (in_grad, small, operands)


def body(
    block_in,
    positions,
    out_grad,
    w_qkv,
    b_qkv,
    w_out,
    b_out,
    w_up,
    b_up,
    w_down,
    b_down,
    first_gain,
    first_shift,
    second_gain,
    second_shift,
):
    gathered = (
        lax.all_gather(w_qkv, "shard", axis=0, tiled=True),
        lax.all_gather(b_qkv, "shard", axis=0, tiled=True),
        lax.all_gather(w_out, "shard", axis=0, tiled=True),
        lax.all_gather(b_out, "shard", axis=0, tiled=True),
        lax.all_gather(w_up, "shard", axis=0, tiled=True),
        lax.all_gather(b_up, "shard", axis=0, tiled=True),
        lax.all_gather(w_down, "shard", axis=0, tiled=True),
        lax.all_gather(b_down, "shard", axis=0, tiled=True),
        lax.all_gather(first_gain, "shard", axis=0, tiled=True),
        lax.all_gather(first_shift, "shard", axis=0, tiled=True),
        lax.all_gather(second_gain, "shard", axis=0, tiled=True),
        lax.all_gather(second_shift, "shard", axis=0, tiled=True),
    )
    block_out, saved = layer_forward(block_in, positions, gathered)
    regathered = (
        lax.all_gather(w_qkv, "shard", axis=0, tiled=True),
        lax.all_gather(b_qkv, "shard", axis=0, tiled=True),
        lax.all_gather(w_out, "shard", axis=0, tiled=True),
        lax.all_gather(b_out, "shard", axis=0, tiled=True),
        lax.all_gather(w_up, "shard", axis=0, tiled=True),
        lax.all_gather(b_up, "shard", axis=0, tiled=True),
        lax.all_gather(w_down, "shard", axis=0, tiled=True),
        lax.all_gather(b_down, "shard", axis=0, tiled=True),
        lax.all_gather(first_gain, "shard", axis=0, tiled=True),
        lax.all_gather(first_shift, "shard", axis=0, tiled=True),
        lax.all_gather(second_gain, "shard", axis=0, tiled=True),
        lax.all_gather(second_shift, "shard", axis=0, tiled=True),
    )
    in_grad, small, operands = layer_backward(saved, out_grad, regathered)
    first_low, mixed_low, attended, second_low, hidden_low, activated = operands
    full_rows = (
        lax.all_gather(mixed_low, "shard", axis=0, tiled=True),
        lax.all_gather(out_grad, "shard", axis=0, tiled=True),
        lax.all_gather(hidden_low, "shard", axis=0, tiled=True),
    )
    own_columns = (
        lax.all_to_all(first_low, "shard", split_axis=1, concat_axis=0, tiled=True),
        lax.all_to_all(attended, "shard", split_axis=1, concat_axis=0, tiled=True),
        lax.all_to_all(second_low, "shard", split_axis=1, concat_axis=0, tiled=True),
        lax.all_to_all(activated, "shard", split_axis=1, concat_axis=0, tiled=True),
    )
    owned_small = (
        lax.psum_scatter(small[0], "shard", scatter_dimension=0, tiled=True),
        lax.psum_scatter(small[1], "shard", scatter_dimension=0, tiled=True),
        lax.psum_scatter(small[2], "shard", scatter_dimension=0, tiled=True),
        lax.psum_scatter(small[3], "shard", scatter_dimension=0, tiled=True),
        lax.psum_scatter(small[4], "shard", scatter_dimension=0, tiled=True),
        lax.psum_scatter(small[5], "shard", scatter_dimension=0, tiled=True),
        lax.psum_scatter(small[6], "shard", scatter_dimension=0, tiled=True),
        lax.psum_scatter(small[7], "shard", scatter_dimension=0, tiled=True),
    )
    owned_qkv = contract_rows(own_columns[0], full_rows[0])
    owned_out = contract_rows(own_columns[1], full_rows[1])
    owned_up = contract_rows(own_columns[2], full_rows[2])
    owned_down = contract_rows(own_columns[3], full_rows[1])
    summed = lax.psum(
        (
            owned_qkv,
            owned_small[0],
            owned_out,
            owned_small[1],
            owned_up,
            owned_small[2],
            owned_down,
            owned_small[3],
            owned_small[4],
            owned_small[5],
            owned_small[6],
            owned_small[7],
        ),
        "replica",
    )
    return (
        block_out,
        in_grad,
        summed[0],
        summed[1],
        summed[2],
        summed[3],
        summed[4],
        summed[5],
        summed[6],
        summed[7],
        summed[8],
        summed[9],
        summed[10],
        summed[11],
    )


def solution(mesh):
    return jax.shard_map(
        body,
        mesh=mesh,
        in_specs=(
            P(("shard", "replica"), None),
            P(("shard", "replica")),
            P(("shard", "replica"), None),
            P("shard", None),
            P("shard"),
            P("shard", None),
            P("shard"),
            P("shard", None),
            P("shard"),
            P("shard", None),
            P("shard"),
            P("shard"),
            P("shard"),
            P("shard"),
            P("shard"),
        ),
        out_specs=(
            P(("shard", "replica"), None),
            P(("shard", "replica"), None),
            P("shard", None),
            P("shard"),
            P("shard", None),
            P("shard"),
            P("shard", None),
            P("shard"),
            P("shard", None),
            P("shard"),
            P("shard"),
            P("shard"),
            P("shard"),
            P("shard"),
        ),
        check_vma=False,
    )
```

profile of v0, /device:TPU:0, one launch (start us, length us, event | category | flops | bytes accessed | tf_op | source)
XLA Modules:
  0.0 2759.7 jit_solution(14352678589043947305)
XLA Ops:
  11.4 13.6 all-gather.5
  25.0 15.0 all-gather.4
  40.6 13.4 all-gather.1
  54.0 20.1 all-gather
  74.1 16.6 all-gather.2
  92.2 70.4 %all-gather.17.cloned.1.call-done = bf16[2048,2048]{1,0:T(8,128)(2,1)} async-done(((bf16[512,2048]{1,0:T(8,128)(2,1)}), bf16[2048,2048]{1,0:T(8,128)(2,1)}) %all-gather.17.cloned.1.call-update) | async-done | bytes 8388624 | tf_op jit(solution)/shard_map/all_gather | solution.py:264
  162.7 6.3 convolution_convert_fusion
  169.2 418.4 %all-gather.15.cloned.1.call-done = bf16[2048,6144]{1,0:T(8,128)(2,1)} async-done(((bf16[512,6144]{1,0:T(8,128)(2,1)}), bf16[2048,6144]{1,0:T(8,128)(2,1)}) %all-gather.15.cloned.1.call-update) | async-done | bytes 25165840 | tf_op jit(solution)/shard_map/all_gather | solution.py:262
  587.7 12.4 convolution_add_fusion.1
  604.6 2.1 convolution_bitcast_fusion
  608.0 3.0 convolution_bitcast_fusion.1
  612.7 3.0 multiply_subtract_fusion.1
  619.0 3.2 pad_maximum_fusion.1
  623.8 1.9 fusion.56
  628.1 33.1 %all_gather.60 = bf16[8192]{0:T(1024)(128)(2,1)S(1)} all-gather(bf16[2048]{0:T(1024)(128)(2,1)S(1)} %copy-done.25), channel_id=1, replica_groups=mesh['shard'=4,'replica'=8] {'shard'}, dimensions={0}, use_global_device_ids=true | all-gather | bytes 20480 | tf_op jit(solution)/shard_map/all_gather | solution.py:267
  661.2 487.9 %all-gather.19.cloned.1.call-done = bf16[2048,8192]{1,0:T(8,128)(2,1)} async-done(((bf16[512,8192]{1,0:T(8,128)(2,1)}), bf16[2048,8192]{1,0:T(8,128)(2,1)}) %all-gather.19.cloned.1.call-update) | async-done | bytes 33554448 | tf_op jit(solution)/shard_map/all_gather | solution.py:266
  1149.1 20.1 multiply_convert_fusion
  1169.2 540.9 %all-gather.21.cloned.1.call-done = bf16[8192,2048]{1,0:T(8,128)(2,1)} async-done(((bf16[2048,2048]{1,0:T(8,128)(2,1)}), bf16[8192,2048]{1,0:T(8,128)(2,1)}) %all-gather.21.cloned.1.call-update) | async-done | bytes 33554448 | tf_op jit(solution)/shard_map/all_gather | solution.py:268
  1710.1 18.9 fusion.67
  1731.7 4.1 all-to-all-start.1
  1735.8 1.9 copy.143
  1737.7 26.8 all-to-all-done.1
  1764.5 4.3 all-to-all-start
  1770.7 3.3 fusion.8
  1774.0 5.4 fusion.74
  1779.5 24.0 all-to-all-done
  1803.5 84.4 %all-gather.23.cloned.1.call-done = bf16[512,6144]{0,1:T(8,128)(2,1)} async-done(((bf16[128,6144]{0,1:T(8,128)(2,1)}), bf16[512,6144]{0,1:T(8,128)(2,1)}) %all-gather.23.cloned.1.call-update) | async-done | bytes 6291472 | tf_op jit(solution)/shard_map/all_gather | solution.py:293
  1887.9 12.0 fusion.73
  1901.3 4.5 all-to-all-start.3
  1905.9 17.3 fusion.72
  1923.2 15.5 fusion.37
  1938.6 3.9 convert_reduce_fusion.1
  1942.6 69.0 %all-to-all-done.3 = bf16[128,4,2048]{2,0,1:T(8,128)(2,1)} async-done(((bf16[128,4,2048]{2,0,1:T(8,128)(2,1)}), bf16[128,4,2048]{2,0,1:T(8,128)(2,1)}, u32[]{:S(2)}, u32[]{:S(2)}) %all-to-all-start.3) | async-done | bytes 2097184 | tf_op jit(solution)/shard_map/all_to_all | solution.py:301
  2011.6 4.4 all-to-all-start.2
  2016.0 13.0 fusion.76
  2029.0 16.0 all-to-all-done.2
  2044.9 50.6 %all-gather.27.cloned.1.call-done = bf16[512,8192]{1,0:T(8,128)(2,1)} async-done(((bf16[128,8192]{1,0:T(8,128)(2,1)}), bf16[512,8192]{1,0:T(8,128)(2,1)}) %all-gather.27.cloned.1.call-update) | async-done | bytes 8388624 | tf_op jit(solution)/shard_map/all_gather | solution.py:295
  2095.5 14.3 fusion.75
  2110.5 11.9 all-gather.3
  2122.5 11.9 all-gather.6
  2137.0 4.7 fusion.6
  2141.7 15.8 fusion.7
  2162.7 24.8 all-reduce.7
  2187.5 529.5 %all-reduce.13.cloned.1.call-done = (f32[512,6144]{1,0:T(8,128)}, f32[512,2048]{1,0:T(8,128)}, f32[512,8192]{1,0:T(8,128)}, f32[2048,2048]{1,0:T(8,128)}) async-done(((f32[512,6144]{1,0:T(8,128)}, f32[512,2048]{1,0:T(8,128)}, f32[512,8192]{1,0:T(8,128)}, f32[2048,2048]{1,0:T(8,128)}), (f32[512,6144]{1,0:T(8,128)}, f32[512,2048]{1,0:T(8,128)}, f32[512,8192]{1,0:T(8,128)}, ...) | async-done | bytes 50331664 | tf_op jit(solution)/shard_map/psum | solution.py:317
  2717.6 11.0 copy.157
  2728.6 2.1 copy.158
  2730.7 13.9 copy.159
  2746.8 6.2 copy.160
  (163 shorter events, 36.2 us)
Async XLA Ops:
  7.2 155.5 %all-gather.17.cloned.1.call-start = ((), (), s32[]{:S(2)}) async-start(), calls=%async_computation.5 | async-start | bytes 10485760 | tf_op jit(solution)/shard_map/all_gather | solution.py:264
  7.9 579.8 %all-gather.15.cloned.1.call-start = ((), (), s32[]{:S(2)}) async-start(), calls=%async_computation.4 | async-start | bytes 31457280 | tf_op jit(solution)/shard_map/all_gather | solution.py:262
  8.7 1140.4 %all-gather.19.cloned.1.call-start = ((), (), s32[]{:S(2)}) async-start(), calls=%async_computation.6 | async-start | bytes 41943040 | tf_op jit(solution)/shard_map/all_gather | solution.py:266
  9.4 1.9 copy-start.28
  9.4 15.6 copy-start.29
  9.4 30.6 %copy-start = (bf16[128,2048]{1,0:T(8,128)(2,1)S(1)}, bf16[128,2048]{1,0:T(8,128)(2,1)}, u32[]{:S(2)}) copy-start(bf16[128,2048]{1,0:T(8,128)(2,1)} %param.15) | copy-start | bytes 1572868
  9.4 31.1 %copy-start.30 = (bf16[512]{0:T(512)(128)(2,1)S(1)}, bf16[512]{0:T(512)(128)(2,1)}, u32[]{:S(2)}) copy-start(bf16[512]{0:T(512)(128)(2,1)} %param.27) | copy-start | bytes 3076
  9.4 44.6 %copy-start.31 = (bf16[512]{0:T(512)(128)(2,1)S(1)}, bf16[512]{0:T(512)(128)(2,1)}, u32[]{:S(2)}) copy-start(bf16[512]{0:T(512)(128)(2,1)} %param.26) | copy-start | bytes 3076
  9.5 64.6 %copy-start.26 = (bf16[1536]{0:T(1024)(128)(2,1)S(1)}, bf16[1536]{0:T(1024)(128)(2,1)}, u32[]{:S(2)}) copy-start(bf16[1536]{0:T(1024)(128)(2,1)} %param.19) | copy-start | bytes 9220
  9.5 153.2 %copy-start.9 = (bf16[128,2048]{1,0:T(8,128)(2,1)S(1)}, bf16[128,2048]{1,0:T(8,128)(2,1)}, u32[]{:S(2)}) copy-start(bf16[128,2048]{1,0:T(8,128)(2,1)} %param.17) | copy-start | bytes 1572868
  9.5 1700.6 %all-gather.21.cloned.1.call-start = ((), (), s32[]{:S(2)}) async-start(), calls=%async_computation.7 | async-start | bytes 41943040 | tf_op jit(solution)/shard_map/all_gather | solution.py:268
  10.1 1764.0 %all-gather.25.cloned.1.call-start = ((), (), s32[]{:S(2)}) async-start(), calls=%async_computation.9 | async-start | bytes 2621440 | tf_op jit(solution)/shard_map/all_gather | solution.py:294
  10.6 1877.2 %all-gather.23.cloned.1.call-start = ((), (), s32[]{:S(2)}) async-start(), calls=%async_computation.8 | async-start | bytes 7864320 | tf_op jit(solution)/shard_map/all_gather | solution.py:293
  40.2 128.7 %copy-start.21 = (f32[128]{0:T(128)}, f32[128]{0:T(128)S(1)}, u32[]{:S(2)}) copy-start(f32[128]{0:T(128)S(1)} %broadcast_multiply_fusion.4) | copy-start | bytes 1540
  40.5 128.4 %copy-start.23 = (f32[128]{0:T(128)}, f32[128]{0:T(128)S(1)}, u32[]{:S(2)}) copy-start(f32[128]{0:T(128)S(1)} %add_rsqrt_fusion) | copy-start | bytes 1540
  92.2 495.5 %copy-start.4 = (bf16[128,2048]{1,0:T(8,128)(2,1)}, bf16[128,2048]{1,0:T(8,128)(2,1)S(1)}, u32[]{:S(2)}) copy-start(bf16[128,2048]{1,0:T(8,128)(2,1)S(1)} %get-tuple-element.61) | copy-start | bytes 1572868
  92.2 1056.9 %copy-start.5 = (bf16[128,2048]{1,0:T(8,128)(2,1)}, bf16[128,2048]{1,0:T(8,128)(2,1)S(1)}, u32[]{:S(2)}) copy-start(bf16[128,2048]{1,0:T(8,128)(2,1)S(1)} %get-tuple-element.60) | copy-start | bytes 1572868
  169.2 435.0 %copy-start.7 = (bf16[128,2048]{0,1:T(8,128)(2,1)}, bf16[128,2048]{0,1:T(8,128)(2,1)S(1)}, u32[]{:S(2)}) copy-start(bf16[128,2048]{0,1:T(8,128)(2,1)S(1)} %copy.103) | copy-start | bytes 1572868
  600.1 4.2 copy-start.6
  601.9 2.4 copy-start.13
  602.0 2.2 copy-start.14
  602.5 1.8 copy-start.15
  602.5 1.8 copy-start.16
  602.5 1.8 copy-start.17
  603.5 7.5 copy-start.8
  606.7 1.3 copy-start.12
  611.0 4.8 copy-start.10
  617.4 6.4 copy-start.19
  619.0 8.9 copy-start.1
  623.8 4.2 copy-start.2
  623.8 4.3 copy-start.25
  628.0 1467.5 %all-gather.27.cloned.1.call-start = ((), (), s32[]{:S(2)}) async-start(), calls=%async_computation.10 | async-start | bytes 10485760 | tf_op jit(solution)/shard_map/all_gather | solution.py:295
  1731.7 32.8 %all-to-all-start.1 = ((bf16[128,4,512]{2,0,1:T(8,128)(2,1)}), bf16[128,4,512]{2,0,1:T(8,128)(2,1)}, u32[]{:S(2)}, u32[]{:S(2)}) async-start(bf16[128,4,512]{2,0,1:T(8,128)(2,1)} %copy.92), calls=%async_computation.1 | async-start | bytes 1048576 | tf_op jit(solution)/shard_map/all_to_all | solution.py:299
  1764.5 39.0 %all-to-all-start = ((bf16[128,4,512]{2,0,1:T(8,128)(2,1)}), bf16[128,4,512]{2,0,1:T(8,128)(2,1)}, u32[]{:S(2)}, u32[]{:S(2)}) async-start(bf16[128,4,512]{2,0,1:T(8,128)(2,1)} %bitcast.112), calls=%async_computation | async-start | bytes 1048576 | tf_op jit(solution)/shard_map/all_to_all | solution.py:298
  1901.3 110.3 %all-to-all-start.3 = ((bf16[128,4,2048]{2,0,1:T(8,128)(2,1)}), bf16[128,4,2048]{2,0,1:T(8,128)(2,1)}, u32[]{:S(2)}, u32[]{:S(2)}) async-start(bf16[128,4,2048]{2,0,1:T(8,128)(2,1)} %bitcast.96), calls=%async_computation.3 | async-start | bytes 4194304 | tf_op jit(solution)/shard_map/all_to_all | solution.py:301
  1905.8 17.4 copy-start.22
  1905.8 17.4 copy-start.24
  1905.8 251.6 %all-reduce.15.cloned.1.call-start = ((), (), s32[]{:S(2)}) async-start(), calls=%async_computation.12 | async-start | bytes 196608
  2011.6 33.3 %all-to-all-start.2 = ((bf16[128,4,512]{2,0,1:T(8,128)(2,1)}), bf16[128,4,512]{2,0,1:T(8,128)(2,1)}, u32[]{:S(2)}, u32[]{:S(2)}) async-start(bf16[128,4,512]{2,0,1:T(8,128)(2,1)} %bitcast.111), calls=%async_computation.2 | async-start | bytes 1048576 | tf_op jit(solution)/shard_map/all_to_all | solution.py:300
  2016.0 701.1 %all-reduce.13.cloned.1.call-start = ((), (), s32[]{:S(2)}) async-start(), calls=%async_computation.11 | async-start | bytes 100663296 | tf_op jit(solution)/shard_map/psum | solution.py:317
  2109.8 12.6 copy-start.33
  2109.8 24.6 copy-start.35
  2187.5 541.1 %copy-start.27 = (f32[512]{0:T(512)}, f32[512]{0:T(512)S(1)}, u32[]{:S(2)}) copy-start(f32[512]{0:T(512)S(1)} %get-tuple-element.112) | copy-start | bytes 6148
  2717.6 11.0 copy-start.11
  2728.6 16.0 slice-start
  2730.7 13.9 slice-start.1
  2730.7 14.4 slice-start.2
  2730.7 16.0 slice-start.3
  (5 other events, 4.8 us)
Sparse Core Ops, SparseCore 0:
  9.6 153.0 all-gather.16
  164.2 423.3 all-gather.14
  589.2 559.8 all-gather.18
  1150.5 559.5 all-gather.20
  1711.5 55.0 all-gather.24
  1768.1 119.7 all-gather.22
  1890.0 205.4 all-gather.26
  2099.0 33.4 all-reduce.14
  2137.8 579.1 all-reduce.12
where the time goes:
time: 2760 us
  waiting for transfers between devices  2320 us (84%)
  matrix products  165 us (6%)
  blocking collectives  160 us (6%)
  local copies, waits for them, and re-layouts  58.2 us (2%)
    all_gather x1, waiting for transfers between devices, body(): lax.all_gather(w_down, 'shard', axis=0, tiled=True)  541 us
    psum x1, waiting for transfers between devices, body(): lax.psum((owned_qkv, owned_small[0], owned_out, owned_small[1], owned_up,...  530 us
    all_gather x1, waiting for transfers between devices, body(): lax.all_gather(w_up, 'shard', axis=0, tiled=True)  488 us
    all_gather x1, waiting for transfers between devices, body(): lax.all_gather(w_qkv, 'shard', axis=0, tiled=True)  418 us
    all_gather x1, waiting for transfers between devices, body(): lax.all_gather(mixed_low, 'shard', axis=0, tiled=True)  84.4 us
    all_gather x1, waiting for transfers between devices, body(): lax.all_gather(w_out, 'shard', axis=0, tiled=True)  70.4 us
    all_to_all x1, waiting for transfers between devices, body(): lax.all_to_all(activated, 'shard', split_axis=1, concat_axis=0, tiled=True)  69 us
    dot_general x4, matrix products, times_transpose(): lax.dot_general(left, right, (((1,), (1,)), ((), ())), preferred_element_...  57.9 us
  transfers between devices with their start and end apart: 13, of which 11 were waited for; matrix products, arithmetic and copies ran while one was open for 7% of the time, Pallas kernels for 0%

commit v1 on v0

--- a/solution.py
+++ b/solution.py
@@ -8,6 +8,27 @@
 HD = 256
 ROT = 64
 epsilon = 1e-05
+
+
+def joined_along(blocks, dim):
+    blocks = jnp.moveaxis(blocks, 0, dim)
+    shape = blocks.shape
+    return blocks.reshape(*shape[:dim], shape[dim] * shape[dim + 1], *shape[dim + 2 :])
+
+
+def grow_blocks(x, axis):
+    length, position = (lax.axis_size(axis), lax.axis_index(axis))
+    parts, bit = (x[None], 1)
+    while bit < length:
+        theirs = lax.ppermute(parts, axis, [(i, i ^ bit) for i in range(length)])
+        low = position & bit == 0
+        parts = jnp.concatenate([jnp.where(low, parts, theirs), jnp.where(low, theirs, parts)])
+        bit *= 2
+    return parts
+
+
+def gather_by_bits(x, axis, dim):
+    return joined_along(grow_blocks(x, axis), dim)
 
 
 def norm_forward(values, gain, shift):
@@ -263,7 +284,7 @@
         lax.all_gather(b_qkv, "shard", axis=0, tiled=True),
         lax.all_gather(w_out, "shard", axis=0, tiled=True),
         lax.all_gather(b_out, "shard", axis=0, tiled=True),
-        lax.all_gather(w_up, "shard", axis=0, tiled=True),
+        gather_by_bits(w_up, "shard", 0),
         lax.all_gather(b_up, "shard", axis=0, tiled=True),
         lax.all_gather(w_down, "shard", axis=0, tiled=True),
         lax.all_gather(b_down, "shard", axis=0, tiled=True),

time: 2760 us -> 3640 us (1.32)
  blocking collectives: 160 us -> 1520 us
  waiting for transfers between devices: 2320 us -> 1780 us
  other arithmetic: 20.2 us -> 79.4 us
    all_gather x1, blocking collectives: 33.1 us -> 1390 us  [body(): lax.all_gather(b_up, 'shard', axis=0, tiled=True)]
    ppermute x0 -> x2, waiting for transfers between devices: none -> 631 us  [grow_blocks(): theirs = lax.ppermute(parts, axis, [(i, i ^ bit) for i in range(length)])]
    all_gather x1, waiting for transfers between devices: 541 us -> 0.01 us  [body(): lax.all_gather(w_down, 'shard', axis=0, tiled=True)]
    all_gather x1, waiting for transfers between devices: 488 us -> 0.01 us  [body(): lax.all_gather(w_up, 'shard', axis=0, tiled=True)]
    all_gather x1, waiting for transfers between devices: 84.4 us -> 0.02 us  [body(): lax.all_gather(mixed_low, 'shard', axis=0, tiled=True)]
    all_gather x1, waiting for transfers between devices: 50.6 us -> 0.02 us  [body(): lax.all_gather(hidden_low, 'shard', axis=0, tiled=True)]
  transfers between devices with their start and end apart: 13 -> 15, of which waited for: 11 -> 7; matrix products, arithmetic and copies ran while one was open for 7% -> 7% of each run, Pallas kernels for 0% -> 0%
where the time goes in v1:
time: 3640 us; the launch traced here: 3630 us
  waiting for transfers between devices  1780 us (49%)
  blocking collectives  1520 us (42%)
  matrix products  159 us (4%)
  other arithmetic  79.4 us (2%)
  local copies, waits for them, and re-layouts  60.3 us (2%)
    all_gather x1, blocking collectives, body(): lax.all_gather(b_up, 'shard', axis=0, tiled=True)  1390 us
    ppermute x2, waiting for transfers between devices, grow_blocks(): theirs = lax.ppermute(parts, axis, [(i, i ^ bit) for i in range(length)])  631 us
    psum x1, waiting for transfers between devices, body(): lax.psum((owned_qkv, owned_small[0], owned_out, owned_small[1], owned_up,...  529 us
    all_gather x1, waiting for transfers between devices, body(): lax.all_gather(w_qkv, 'shard', axis=0, tiled=True)  418 us
    all_to_all x1, waiting for transfers between devices, body(): lax.all_to_all(activated, 'shard', split_axis=1, concat_axis=0, tiled=True)  98.5 us
  transfers between devices with their start and end apart: 15, of which 7 were waited for; matrix products, arithmetic and copies ran while one was open for 7% of the time, Pallas kernels for 0%

profile of v1, /device:TPU:0, one launch (start us, length us, event | category | flops | bytes accessed | tf_op | source)
XLA Modules:
  0.0 3632.1 jit_solution(17133252221766404275)
XLA Ops:
  10.8 13.6 all-gather.5
  24.4 15.7 all-gather.4
  40.7 13.3 all-gather.1
  54.0 20.0 all-gather
  74.1 16.6 all-gather.2
  92.2 70.4 %all-gather.17.cloned.1.call-done = bf16[2048,2048]{1,0:T(8,128)(2,1)} async-done(((bf16[512,2048]{1,0:T(8,128)(2,1)}), bf16[2048,2048]{1,0:T(8,128)(2,1)}) %all-gather.17.cloned.1.call-update) | async-done | bytes 8388624 | tf_op jit(solution)/shard_map/all_gather | solution.py:285
  162.6 6.3 convolution_convert_fusion
  169.2 418.4 %all-gather.15.cloned.1.call-done = bf16[2048,6144]{1,0:T(8,128)(2,1)} async-done(((bf16[512,6144]{1,0:T(8,128)(2,1)}), bf16[2048,6144]{1,0:T(8,128)(2,1)}) %all-gather.15.cloned.1.call-update) | async-done | bytes 25165840 | tf_op jit(solution)/shard_map/all_gather | solution.py:283
  587.6 12.8 convolution_add_fusion.1
  605.0 2.1 convolution_bitcast_fusion
  608.4 3.0 convolution_bitcast_fusion.1
  613.2 3.0 multiply_subtract_fusion.1
  619.4 3.2 pad_maximum_fusion.3
  624.1 1.9 fusion.56
  629.1 631.3 %collective-permute-done = bf16[1,512,8192]{2,1,0:T(8,128)(2,1)} collective-permute-done((bf16[1,512,8192]{2,1,0:T(8,128)(2,1)}, bf16[1,512,8192]{2,1,0:T(8,128)(2,1)}, u32[]{:S(2)}, u32[]{:S(2)}) %collective-permute-start) | collective-permute-done | bytes 8388640 | tf_op jit(solution)/shard_map/ppermute | solution.py:23
  1260.4 6.5 broadcast_select_fusion.3
  1266.9 9.1 pad_maximum_fusion.1
  1276.0 2.1 copy-done.1
  1278.1 1388.1 %all_gather.58 = bf16[8192]{0:T(1024)(128)(2,1)S(1)} all-gather(bf16[2048]{0:T(1024)(128)(2,1)S(1)} %copy-done.31), channel_id=1, replica_groups=mesh['shard'=4,'replica'=8] {'shard'}, dimensions={0}, use_global_device_ids=true | all-gather | bytes 20480 | tf_op jit(solution)/shard_map/all_gather | solution.py:288
  2666.2 22.6 broadcast_select_fusion.1
  2688.8 22.9 pad_maximum_fusion
  2711.7 15.3 multiply_convert_fusion
  2727.0 18.9 fusion.67
  2747.4 5.3 all-to-all-start.3
  2755.4 98.5 %all-to-all-done.3 = bf16[128,4,2048]{2,0,1:T(8,128)(2,1)} async-done(((bf16[128,4,2048]{2,0,1:T(8,128)(2,1)}), bf16[128,4,2048]{2,0,1:T(8,128)(2,1)}, u32[]{:S(2)}, u32[]{:S(2)}) %all-to-all-start.3) | async-done | bytes 2097184 | tf_op jit(solution)/shard_map/all_to_all | solution.py:322
  2853.8 4.1 all-to-all-start.1
  2859.9 1.9 copy.142
  2861.8 22.3 all-to-all-done.1
  2884.1 4.4 all-to-all-start
  2888.5 13.1 fusion.76
  2903.1 4.4 fusion.74
  2907.5 7.6 all-to-all-done
  2915.1 4.1 all-to-all-start.2
  2919.3 11.2 fusion.73
  2930.6 17.6 fusion.72
  2948.2 15.4 fusion.37
  2963.6 3.9 convert_reduce_fusion.1
  2967.6 14.3 fusion.75
  2982.6 12.4 all-gather.3
  2995.0 11.9 all-gather.6
  3009.5 4.7 fusion.6
  3014.2 15.6 fusion.7
  3035.0 24.8 all-reduce.7
  3059.9 529.3 %all-reduce.13.cloned.1.call-done = (f32[512,6144]{1,0:T(8,128)}, f32[512,2048]{1,0:T(8,128)}, f32[512,8192]{1,0:T(8,128)}, f32[2048,2048]{1,0:T(8,128)}) async-done(((f32[512,6144]{1,0:T(8,128)}, f32[512,2048]{1,0:T(8,128)}, f32[512,8192]{1,0:T(8,128)}, f32[2048,2048]{1,0:T(8,128)}), (f32[512,6144]{1,0:T(8,128)}, f32[512,2048]{1,0:T(8,128)}, f32[512,8192]{1,0:T(8,128)}, ...) | async-done | bytes 50331664 | tf_op jit(solution)/shard_map/psum | solution.py:338
  3589.8 11.0 copy.157
  3600.8 2.1 copy.158
  3602.9 13.9 copy.159
  3618.9 6.2 copy.160
  (183 shorter events, 37.9 us)
Async XLA Ops:
  7.2 155.4 %all-gather.17.cloned.1.call-start = ((), (), s32[]{:S(2)}) async-start(), calls=%async_computation.5 | async-start | bytes 10485760 | tf_op jit(solution)/shard_map/all_gather | solution.py:285
  7.9 16.5 copy-start.35
  7.9 32.2 copy-start.2
  8.0 579.7 %all-gather.15.cloned.1.call-start = ((), (), s32[]{:S(2)}) async-start(), calls=%async_computation.4 | async-start | bytes 31457280 | tf_op jit(solution)/shard_map/all_gather | solution.py:283
  8.7 32.0 copy-start.36
  8.7 45.3 %copy-start.37 = (bf16[512]{0:T(512)(128)(2,1)S(1)}, bf16[512]{0:T(512)(128)(2,1)}, u32[]{:S(2)}) copy-start(bf16[512]{0:T(512)(128)(2,1)} %param.26) | copy-start | bytes 3076
  8.7 65.4 %copy-start.32 = (bf16[1536]{0:T(1024)(128)(2,1)S(1)}, bf16[1536]{0:T(1024)(128)(2,1)}, u32[]{:S(2)}) copy-start(bf16[1536]{0:T(1024)(128)(2,1)} %param.19) | copy-start | bytes 9220
  8.7 153.9 %copy-start.14 = (bf16[128,2048]{1,0:T(8,128)(2,1)S(1)}, bf16[128,2048]{1,0:T(8,128)(2,1)}, u32[]{:S(2)}) copy-start(bf16[128,2048]{1,0:T(8,128)(2,1)} %param.17) | copy-start | bytes 1572868
  8.7 2718.3 %all-gather.19.cloned.1.call-start = ((), (), s32[]{:S(2)}) async-start(), calls=%async_computation.6 | async-start | bytes 41943040 | tf_op jit(solution)/shard_map/all_gather | solution.py:289
  9.5 2879.0 %all-gather.25.cloned.1.call-start = ((), (), s32[]{:S(2)}) async-start(), calls=%async_computation.9 | async-start | bytes 2621440 | tf_op jit(solution)/shard_map/all_gather | solution.py:315
  10.1 2909.3 %all-gather.23.cloned.1.call-start = ((), (), s32[]{:S(2)}) async-start(), calls=%async_computation.8 | async-start | bytes 7864320 | tf_op jit(solution)/shard_map/all_gather | solution.py:314
  40.4 128.8 %copy-start.27 = (f32[128]{0:T(128)}, f32[128]{0:T(128)S(1)}, u32[]{:S(2)}) copy-start(f32[128]{0:T(128)S(1)} %broadcast_multiply_fusion.4) | copy-start | bytes 1540
  40.7 559.8 %copy-start.29 = (f32[128]{0:T(128)}, f32[128]{0:T(128)S(1)}, u32[]{:S(2)}) copy-start(f32[128]{0:T(128)S(1)} %add_rsqrt_fusion) | copy-start | bytes 1540
  92.2 508.2 %copy-start.9 = (bf16[128,2048]{1,0:T(8,128)(2,1)}, bf16[128,2048]{1,0:T(8,128)(2,1)S(1)}, u32[]{:S(2)}) copy-start(bf16[128,2048]{1,0:T(8,128)(2,1)S(1)} %get-tuple-element.65) | copy-start | bytes 1572868
  92.2 2619.5 %copy-start.10 = (bf16[128,2048]{1,0:T(8,128)(2,1)}, bf16[128,2048]{1,0:T(8,128)(2,1)S(1)}, u32[]{:S(2)}) copy-start(bf16[128,2048]{1,0:T(8,128)(2,1)S(1)} %get-tuple-element.64) | copy-start | bytes 1572868
  169.2 435.5 %copy-start.13 = (bf16[128,2048]{0,1:T(8,128)(2,1)}, bf16[128,2048]{0,1:T(8,128)(2,1)S(1)}, u32[]{:S(2)}) copy-start(bf16[128,2048]{0,1:T(8,128)(2,1)S(1)} %copy.103) | copy-start | bytes 1572868
  603.9 12.3 copy-start.12
  611.4 4.8 copy-start.15
  616.2 7.9 copy-start.25
  619.4 9.0 copy-start.3
  624.1 4.8 copy-start.5
  628.4 2302.2 %all-gather.21.cloned.1.call-start = ((), (), s32[]{:S(2)}) async-start(), calls=%async_computation.7 | async-start | bytes 41943040 | tf_op jit(solution)/shard_map/all_gather | solution.py:302
  628.9 2338.7 %all-gather.27.cloned.1.call-start = ((), (), s32[]{:S(2)}) async-start(), calls=%async_computation.10 | async-start | bytes 10485760 | tf_op jit(solution)/shard_map/all_gather | solution.py:316
  629.0 631.4 %collective-permute-start = (bf16[1,512,8192]{2,1,0:T(8,128)(2,1)}, bf16[1,512,8192]{2,1,0:T(8,128)(2,1)}, u32[]{:S(2)}, u32[]{:S(2)}) collective-permute-start(bf16[1,512,8192]{2,1,0:T(8,128)(2,1)} %bitcast.92), channel_id=1, source_target_pairs={{0,8},{8,0},{16,24},{24,16},{1,9},{9,1},{17,25},{25,17},{2,10},{10... | collective-permute-start | bytes 25165832 | tf_op jit(solution)/shard_map/ppermute | solution.py:23
  1266.9 9.1 copy-start
  1266.9 11.2 copy-start.1
  1266.9 11.2 copy-start.31
  1278.1 1388.1 %collective-permute-start.1 = (bf16[2,512,8192]{2,1,0:T(8,128)(2,1)}, bf16[2,512,8192]{2,1,0:T(8,128)(2,1)}, u32[]{:S(2)}, u32[]{:S(2)}) collective-permute-start(bf16[2,512,8192]{2,1,0:T(8,128)(2,1)} %pad_maximum_fusion.1), channel_id=1, source_target_pairs={{0,16},{8,24},{16,0},{24,8},{1,17},{9,25},{17,1},{25,9},{2,18},{10... | collective-permute-start | bytes 50331656 | tf_op jit(solution)/shard_map/ppermute | solution.py:23
  2747.4 106.4 %all-to-all-start.3 = ((bf16[128,4,2048]{2,0,1:T(8,128)(2,1)}), bf16[128,4,2048]{2,0,1:T(8,128)(2,1)}, u32[]{:S(2)}, u32[]{:S(2)}) async-start(bf16[128,4,2048]{2,0,1:T(8,128)(2,1)} %bitcast.102), calls=%async_computation.3 | async-start | bytes 4194304 | tf_op jit(solution)/shard_map/all_to_all | solution.py:322
  2853.8 30.2 all-to-all-start.1
  2884.1 31.0 all-to-all-start
  2888.5 13.1 copy-start.4
  2888.5 13.1 copy-start.6
  2888.5 13.1 copy-start.8
  2888.5 14.6 copy-start.18
  2915.1 52.5 %all-to-all-start.2 = ((bf16[128,4,512]{2,0,1:T(8,128)(2,1)}), bf16[128,4,512]{2,0,1:T(8,128)(2,1)}, u32[]{:S(2)}, u32[]{:S(2)}) async-start(bf16[128,4,512]{2,0,1:T(8,128)(2,1)} %bitcast.117), calls=%async_computation.2 | async-start | bytes 1048576 | tf_op jit(solution)/shard_map/all_to_all | solution.py:321
  2919.3 110.5 %all-reduce.15.cloned.1.call-start = ((), (), s32[]{:S(2)}) async-start(), calls=%async_computation.12 | async-start | bytes 196608
  2930.6 17.6 copy-start.28
  2930.6 17.6 copy-start.30
  2967.5 621.7 %all-reduce.13.cloned.1.call-start = ((), (), s32[]{:S(2)}) async-start(), calls=%async_computation.11 | async-start | bytes 100663296 | tf_op jit(solution)/shard_map/psum | solution.py:338
  2981.9 13.1 copy-start.39
  2981.9 25.0 copy-start.41
  3059.9 540.9 %copy-start.33 = (f32[512]{0:T(512)}, f32[512]{0:T(512)S(1)}, u32[]{:S(2)}) copy-start(f32[512]{0:T(512)S(1)} %get-tuple-element.116) | copy-start | bytes 6148
  3589.8 11.0 copy-start.16
  3600.8 16.0 slice-start
  3602.9 13.9 slice-start.1
  3602.9 14.4 slice-start.2
  3602.9 16.0 slice-start.3
  (13 other events, 25.6 us)
Sparse Core Ops, SparseCore 0:
  9.6 153.0 all-gather.16
  164.2 423.3 all-gather.14
  589.2 780.0 all-gather.18
  1370.7 367.7 all-gather.24
  1739.9 163.5 all-gather.22
  1904.9 793.4 all-gather.20
  2746.1 220.7 all-gather.26
  2970.3 34.1 all-reduce.14
  3010.0 579.1 all-reduce.12
